TPU v7x, 32 devices: a whole 2x2x4 slice. The times are simulated.
32 devices in a mesh: inst: 4 (over x, core), blk: 8 (over z, y).
Axes of the slice: x: 2, y: 2, z: 4, core: 2. Of those that a mesh axis runs over, the one named last changes fastest.
Arguments:
- state: float32 [16, 5, 16, 64, 256], P('inst', None, None, 'blk'), may hold values from -0.53 to 3.9, as said below
- multiples: int32 [7], replicated, may hold values from 1 to 4
Outputs:
- state_change: float32 [16, 5, 16, 64, 256], P('inst', None, None, 'blk')
Inputs may be any that keep to these rules, and one draw needn't show every extreme that they name: `state`: density and pressure lie in 0.7 to 1.3, the axial velocity in 0.2 to 0.8 and the other two velocity components in -0.4 to 0.4; the last variable is the total energy p / 0.4 + rho (u u + v v + w w) / 2.
All inputs are finite; a program needn't handle non-finite values.
Results may differ from a plain program's by a relative error of at most 0.0003.
Values sent between devices are 32-bit elements; how exact they have to be, the bound alone decides.
No kernel may reach another device: no remote copies, remote signals or barrier semaphores. Data moves between devices by JAX's collectives and lax.ppermute only.
A program may use at most 128 MiB of HBM per device.

v0:
```python
import math
import jax
import jax.numpy as jnp
from jax import lax
from jax.sharding import PartitionSpec as P

NT = 16
heat_ratio = 1.4
segment_step = 0.05
smooth_weight = 0.5
base_rate = 0.5
diagonal_weight = 3.0


def extended_2(cells, sides, width):
    for axis, dim in sides:
        count = lax.axis_size(axis)
        head = lax.slice_in_dim(cells, 0, width, axis=dim)
        tail = lax.slice_in_dim(cells, cells.shape[dim] - width, cells.shape[dim], axis=dim)
        cells = jnp.concatenate(
            [
                lax.ppermute(tail, axis, [(i, (i + 1) % count) for i in range(count)]),
                cells,
                lax.ppermute(head, axis, [((i + 1) % count, i) for i in range(count)]),
            ],
            axis=dim,
        )
    return cells


def limited(lower, upper):
    return jnp.maximum(0.0, jnp.minimum(lower, upper)) + jnp.minimum(0.0, jnp.maximum(lower, upper))


def take_part(array_in, offset, amount, along):
    return lax.slice_in_dim(array_in, offset, offset + amount, axis=along)


def primitive(conserved):
    density = conserved[:, 0]
    velocity = [conserved[:, 1] / density, conserved[:, 2] / density, conserved[:, 3] / density]
    kinetic = (
        0.5
        * density
        * (velocity[0] * velocity[0] + velocity[1] * velocity[1] + velocity[2] * velocity[2])
    )
    pressure = (heat_ratio - 1.0) * (conserved[:, 4] - kinetic)
    return [density] + velocity + [pressure]


def physical(states, normal):
    density = states[0]
    pressure = states[4]
    velocity = states[1:4]
    normal_speed = velocity[normal]
    energy = pressure / (heat_ratio - 1.0) + 0.5 * density * (
        velocity[0] * velocity[0] + velocity[1] * velocity[1] + velocity[2] * velocity[2]
    )
    conserved = [
        density,
        density * velocity[0],
        density * velocity[1],
        density * velocity[2],
        energy,
    ]
    flux = [density * normal_speed]
    for member in range(3):
        momentum = density * normal_speed * velocity[member]
        if member == normal:
            momentum = momentum + pressure
        flux.append(momentum)
    flux.append((energy + pressure) * normal_speed)
    wave_speed = jnp.abs(normal_speed) + jnp.sqrt(heat_ratio * pressure / density)
    return (flux, conserved, wave_speed)


def divergence(states, along, normal):
    extent = states[0].shape[along]
    interior = extent - 4
    left_side = []
    right_side = []
    for component in states:
        differences = take_part(component, 1, extent - 1, along) - take_part(
            component, 0, extent - 1, along
        )
        slopes = limited(
            take_part(differences, 0, interior + 2, along),
            take_part(differences, 1, interior + 2, along),
        )
        centres = take_part(component, 1, interior + 2, along)
        left_side.append(
            take_part(centres, 0, interior + 1, along)
            + 0.5 * take_part(slopes, 0, interior + 1, along)
        )
        right_side.append(
            take_part(centres, 1, interior + 1, along)
            - 0.5 * take_part(slopes, 1, interior + 1, along)
        )
    left_flux, left_cons, left_speed = physical(left_side, normal)
    right_flux, right_cons, right_speed = physical(right_side, normal)
    wave_speed = jnp.maximum(left_speed, right_speed)
    result = []
    for member in range(5):
        face_flux = 0.5 * (left_flux[member] + right_flux[member]) - 0.5 * wave_speed * (
            right_cons[member] - left_cons[member]
        )
        result.append(
            take_part(face_flux, 1, interior, along) - take_part(face_flux, 0, interior, along)
        )
    return result


def residual(extended):
    states = primitive(extended)
    inner = [component[:, :, 2:-2, :] for component in states]
    circum = divergence(states, 2, 1)
    axial = divergence(
        [jnp.pad(component, ((0, 0), (2, 2), (0, 0), (0, 0)), mode="edge") for component in inner],
        1,
        0,
    )
    radial = divergence(
        [jnp.pad(component, ((0, 0), (0, 0), (0, 0), (2, 2)), mode="edge") for component in inner],
        3,
        2,
    )
    return jnp.stack(
        [axial[member] + circum[member] + radial[member] for member in range(5)], axis=1
    )


def transform_tables(instances):
    indices = jnp.arange(instances, dtype=jnp.int32)
    harmonic = jnp.where(indices < 2, indices * (instances // 2), indices // 2)
    phases = harmonic[:, None] * indices[None, :] % instances
    angles = phases.astype(jnp.float32) * (2.0 * math.pi / instances)
    sine_rows = (indices % 2 == 1) & (indices >= 2)
    basis = jnp.where(sine_rows[:, None], jnp.sin(angles), jnp.cos(angles))
    weights = jnp.where(indices < 2, 1.0 / instances, 2.0 / instances).astype(jnp.float32)
    return (basis * weights[:, None], basis.T)


def pair_solve(right, frequency):
    cosine_part = right[:, 0]
    sine_part = right[:, 1]
    determinant = diagonal_weight * diagonal_weight + frequency * frequency
    return jnp.stack(
        [
            (diagonal_weight * cosine_part - frequency * sine_part) / determinant,
            (diagonal_weight * sine_part + frequency * cosine_part) / determinant,
        ],
        axis=1,
    )


def neighbours(extended):
    circum = extended[:, :, :, :, :-2] + extended[:, :, :, :, 2:]
    middle = extended[:, :, :, :, 1:-1]
    padded = jnp.pad(middle, ((0, 0), (0, 0), (0, 0), (0, 0), (0, 0), (1, 1)))
    return circum + (padded[:, :, :, :, :, :-2] + padded[:, :, :, :, :, 2:])


def body(state, multiples):
    extended = extended_2(state, (("blk", 3),), 2)
    first_sweep = residual(extended)
    segmented = state - segment_step * first_sweep
    segmented_ext = extended_2(segmented, (("blk", 3),), 2)
    second_sweep = residual(segmented_ext)
    state_freq, residual_freq = (
        lax.all_to_all(state, "inst", split_axis=2, concat_axis=0, tiled=True),
        lax.all_to_all(second_sweep, "inst", split_axis=2, concat_axis=0, tiled=True),
    )
    forward, inverse = transform_tables(NT)
    layout = residual_freq.shape
    paired = (NT // 2, 2) + layout[1:]
    residual_hat = jnp.dot(
        forward, residual_freq.reshape(NT, -1), precision=lax.Precision.HIGHEST
    ).reshape(paired)
    state_hat = jnp.dot(
        forward, state_freq.reshape(NT, -1), precision=lax.Precision.HIGHEST
    ).reshape(paired)
    frequency = jnp.concatenate(
        [jnp.zeros((1,), jnp.float32), base_rate * multiples.astype(jnp.float32)]
    ).reshape(NT // 2, 1, 1, 1, 1)
    source = jnp.stack([frequency * state_hat[:, 1], -frequency * state_hat[:, 0]], axis=1)
    right_hand = -(residual_hat + source)
    widened = extended_2(right_hand, (("blk", 4),), 3)
    correction = pair_solve(widened, frequency)
    for repeat in range(3):
        trimmed = lax.slice_in_dim(widened, repeat + 1, widened.shape[4] - repeat - 1, axis=4)
        correction = pair_solve(trimmed + smooth_weight * neighbours(correction), frequency)
    change_freq = jnp.dot(
        inverse, correction.reshape(NT, -1), precision=lax.Precision.HIGHEST
    ).reshape(layout)
    return lax.all_to_all(change_freq, "inst", split_axis=0, concat_axis=2, tiled=True)


def solution(mesh):
    return jax.shard_map(
        body,
        mesh=mesh,
        in_specs=(P("inst", None, None, "blk", None), P()),
        out_specs=P("inst", None, None, "blk", None),
        check_vma=False,
    )
```

profile of v0, /device:TPU:0, one launch (start us, length us, event | category | flops | bytes accessed | tf_op | source)
XLA Modules:
  0.0 393.5 jit_solution(17723114507473512996)
XLA Ops:
  0.0 3.2 fusion.217
  3.2 3.0 collective-permute-start
  6.2 3.1 collective-permute-start.1
  9.3 24.9 %collective-permute-done = f32[4,5,16,2,256]{4,3,0,2,1:T(2,128)S(1)} collective-permute-done((f32[4,5,16,2,256]{4,3,0,2,1:T(2,128)S(1)}, f32[4,5,16,2,256]{4,3,0,2,1:T(2,128)S(1)}, u32[]{:S(2)}, u32[]{:S(2)}) %collective-permute-start) | collective-permute-done | bytes 655392 | tf_op jit(solution)/shard_map/ppermute | solution.py:22
  34.3 2.2 collective-permute-done.1
  40.3 2.9 multiply_subtract_fusion.26
  94.3 4.1 %multiply_subtract_fusion.16 = (f32[4,16,8,257]{3,2,0,1:T(8,128)S(1)}, f32[4,16,8,257]{3,2,0,1:T(8,128)S(1)}, f32[4,16,8,257]{3,2,0,1:T(8,128)S(1)}, f32[4,16,8,257]{3,2,0,1:T(8,128)S(1)}, f32[4,16,8,257]{3,2,0,1:T(8,128)S(1)}) fusion(f32[4,16,8,258]{3,2,0,1:T(8,128)S(1)} %copy-done.26, f32[4,16,8,256]{3,2,0,1:T(8,128)S(1)} %copy-done.34, ...), kind=kLoop, calls=%fused_computation.254 | loop fusion | flops 8816128 | bytes 10557440 | tf_op jit(solution)/shard_map/sub | solution.py:104
  107.6 3.5 multiply_subtract_fusion.6
  111.2 2.4 multiply_subtract_fusion.7
  119.5 4.4 %collective-permute-start.3 = (f32[4,5,16,2,256]{4,3,0,2,1:T(2,128)}, f32[4,5,16,2,256]{4,3,0,2,1:T(2,128)}, u32[]{:S(2)}, u32[]{:S(2)}) collective-permute-start(f32[4,5,16,2,256]{4,3,0,2,1:T(2,128)} %get-tuple-element.74), channel_id=1, source_target_pairs={{1,0},{2,1},{3,2},{4,3},{5,4},{6,5},{7,6},{0,7},{9,8},{10,9},{11,1... | collective-permute-start | bytes 1966088 | tf_op jit(solution)/shard_map/ppermute | solution.py:24
  125.7 4.5 %all-to-all-start.1 = ((f32[4,5,16,8,256]{4,3,1,0,2:T(8,128)}), f32[4,5,16,8,256]{4,3,1,0,2:T(8,128)}, u32[]{:S(2)}, u32[]{:S(2)}) async-start(f32[4,5,16,8,256]{4,3,1,0,2:T(8,128)} %copy.120), calls=%async_computation.1 | async-start | bytes 5242880 | tf_op jit(solution)/shard_map/all_to_all | solution.py:170
  130.3 16.7 %collective-permute-done.2 = f32[4,5,16,2,256]{4,3,0,2,1:T(2,128)S(1)} collective-permute-done((f32[4,5,16,2,256]{4,3,0,2,1:T(2,128)}, f32[4,5,16,2,256]{4,3,0,2,1:T(2,128)S(1)}, u32[]{:S(2)}, u32[]{:S(2)}) %collective-permute-start.2) | collective-permute-done | bytes 655392 | tf_op jit(solution)/shard_map/ppermute | solution.py:22
  147.0 3.9 collective-permute-done.3
  150.9 2.1 pad_maximum_fusion.1
  161.2 2.6 multiply_subtract_fusion.21
  217.7 4.0 %multiply_subtract_fusion.11 = (f32[4,16,8,257]{3,2,0,1:T(8,128)S(1)}, f32[4,16,8,257]{3,2,0,1:T(8,128)S(1)}, f32[4,16,8,257]{3,2,0,1:T(8,128)S(1)}, f32[4,16,8,257]{3,2,0,1:T(8,128)S(1)}, f32[4,16,8,257]{3,2,0,1:T(8,128)S(1)}) fusion(f32[4,16,8,258]{3,2,0,1:T(8,128)S(1)} %minimum_add_fusion.11, f32[4,16,8,256]{3,2,0,1:T(8,128)S(1)} %copy-done.32, ...), kind=kLoop, calls=%fused_computation.243 | loop fusion | flops 8816128 | bytes 10557440 | tf_op jit(solution)/shard_map/sub | solution.py:104
  228.7 4.3 %multiply_subtract_fusion.1 = (f32[4,16,9,256]{3,2,0,1:T(8,128)S(1)}, f32[4,16,9,256]{3,2,0,1:T(8,128)S(1)}, f32[4,16,9,256]{3,2,0,1:T(8,128)S(1)}, f32[4,16,9,2...) fusion(f32[4,16,10,256]{3,2,0,1:T(8,128)S(1)} %minimum_add_fusion.1, ...), kind=kLoop, calls=%fused_computation.141 | loop fusion | flops 8404992 | bytes 15335424 | tf_op jit(solution)/shard_map/sub | solution.py:104
  233.0 3.3 multiply_subtract_fusion.2
  244.7 4.0 %all-to-all-start = ((f32[4,5,16,8,256]{4,3,0,1,2:T(8,128)}), f32[4,5,16,8,256]{4,3,0,1,2:T(8,128)S(1)}, u32[]{:S(2)}, u32[]{:S(2)}) async-start(f32[4,5,16,8,256]{4,3,0,1,2:T(8,128)} %copy.116), calls=%async_computation | async-start | bytes 5242880 | tf_op jit(solution)/shard_map/all_to_all | solution.py:171
  248.9 3.6 copy.151
  252.5 3.1 reshape.409
  255.6 2.5 copy.131
  258.1 3.7 fusion.22
  261.8 2.0 slice_multiply_fusion.1
  263.8 16.2 %all-to-all-done = f32[4,5,16,8,256]{4,3,0,1,2:T(8,128)S(1)} async-done(((f32[4,5,16,8,256]{4,3,0,1,2:T(8,128)}), f32[4,5,16,8,256]{4,3,0,1,2:T(8,128)S(1)}, u32[]{:S(2)}, u32[]{:S(2)}) %all-to-all-start) | async-done | bytes 2621472 | tf_op jit(solution)/shard_map/all_to_all | solution.py:171
  285.5 3.9 fusion.21
  289.8 5.1 %collective-permute-start.5 = (f32[8,2,5,4,3,256]{5,0,4,3,2,1:T(8,128)S(1)}, f32[8,2,5,4,3,256]{5,0,4,3,2,1:T(8,128)S(1)}, u32[]{:S(2)}, u32[]{:S(2)}) collective-permute-start(f32[8,2,5,4,3,256]{5,0,4,3,2,1:T(8,128)S(1)} %get-tuple-element.72), channel_id=1, source_target_pairs={{1,0},{2,1},{3,2},{4,3},{5,4},{6,5},{7,6},{0,7},{9,8},{10,9},{11,1... | collective-permute-start | bytes 2949128 | tf_op jit(solution)/shard_map/ppermute | solution.py:24
  294.9 36.9 %collective-permute-done.4 = f32[8,2,5,4,3,256]{5,0,4,3,2,1:T(8,128)S(1)} collective-permute-done((f32[8,2,5,4,3,256]{5,0,4,3,2,1:T(8,128)S(1)}, f32[8,2,5,4,3,256]{5,0,4,3,2,1:T(8,128)S(1)}, u32[]{:S(2)}, u32[]{:S(2)}) %collective-permute-start.4) | collective-permute-done | bytes 983072 | tf_op jit(solution)/shard_map/ppermute | solution.py:22
  331.8 3.5 collective-permute-done.5
  350.1 2.5 copy.132
  352.6 3.6 fusion.26
  357.8 33.8 %all_to_all.48 = f32[16,5,4,8,256]{4,3,2,1,0:T(8,128)S(1)} all-to-all(f32[16,5,4,8,256]{4,3,2,1,0:T(8,128)S(1)} %copy.125), channel_id=1, replica_groups=mesh['inst'=4,'blk'=8] {'inst'}, dimensions={0} | all-to-all | bytes 5242880 | tf_op jit(solution)/shard_map/all_to_all | solution.py:195
  (454 shorter events, 171.2 us)
Async XLA Ops:
  0.0 36.5 %copy-start.18 = (f32[4,5,16,8,256]{4,3,2,1,0:T(8,128)S(1)}, f32[4,5,16,8,256]{4,3,2,1,0:T(8,128)}, u32[]{:S(2)}) copy-start(f32[4,5,16,8,256]{4,3,2,1,0:T(8,128)} %param.2) | copy-start | bytes 7864324
  3.2 31.1 %collective-permute-start = (f32[4,5,16,2,256]{4,3,0,2,1:T(2,128)S(1)}, f32[4,5,16,2,256]{4,3,0,2,1:T(2,128)S(1)}, u32[]{:S(2)}, u32[]{:S(2)}) collective-permute-start(f32[4,5,16,2,256]{4,3,0,2,1:T(2,128)S(1)} %get-tuple-element.75), channel_id=1, source_target_pairs={{0,1},{1,2},{2,3},{3,4},{4,5},{5,6},{6,7},{7,0},{8,9},{9,10},{10,1... | collective-permute-start | bytes 1966088 | tf_op jit(solution)/shard_map/ppermute | solution.py:22
  6.2 30.2 %collective-permute-start.1 = (f32[4,5,16,2,256]{4,3,0,2,1:T(2,128)S(1)}, f32[4,5,16,2,256]{4,3,0,2,1:T(2,128)S(1)}, u32[]{:S(2)}, u32[]{:S(2)}) collective-permute-start(f32[4,5,16,2,256]{4,3,0,2,1:T(2,128)S(1)} %get-tuple-element.76), channel_id=1, source_target_pairs={{1,0},{2,1},{3,2},{4,3},{5,4},{6,5},{7,6},{0,7},{9,8},{10,9},{11,1... | collective-permute-start | bytes 1966088 | tf_op jit(solution)/shard_map/ppermute | solution.py:24
  38.3 9.3 %copy-start.10 = (f32[4,16,12,256]{3,2,0,1:T(8,128)}, f32[4,16,12,256]{3,2,0,1:T(8,128)S(1)}, u32[]{:S(2)}) copy-start(f32[4,16,12,256]{3,2,0,1:T(8,128)S(1)} %get-tuple-element.45) | copy-start | bytes 2359300
  38.4 4.8 %copy-start.29 = (f32[4,16,8,256]{3,2,0,1:T(8,128)}, f32[4,16,8,256]{3,2,0,1:T(8,128)S(1)}, u32[]{:S(2)}) copy-start(f32[4,16,8,256]{3,2,0,1:T(8,128)S(1)} %slice.1936) | copy-start | bytes 1572868
  38.5 6.3 %copy-start.22 = (f32[4,16,8,256]{3,2,0,1:T(8,128)}, f32[4,16,8,256]{3,2,0,1:T(8,128)S(1)}, u32[]{:S(2)}) copy-start(f32[4,16,8,256]{3,2,0,1:T(8,128)S(1)} %slice.1978) | copy-start | bytes 1572868
  38.6 6.2 %copy-start.4 = (f32[4,16,8,256]{3,2,0,1:T(8,128)}, f32[4,16,8,256]{3,2,0,1:T(8,128)S(1)}, u32[]{:S(2)}) copy-start(f32[4,16,8,256]{3,2,0,1:T(8,128)S(1)} %slice.1892) | copy-start | bytes 1572868
  38.9 10.0 %copy-start.14 = (f32[4,16,12,256]{3,2,0,1:T(8,128)}, f32[4,16,12,256]{3,2,0,1:T(8,128)S(1)}, u32[]{:S(2)}) copy-start(f32[4,16,12,256]{3,2,0,1:T(8,128)S(1)} %slice_bitcast_fusion.9) | copy-start | bytes 2359300
  39.2 5.6 %copy-start.8 = (f32[4,18,8,256]{3,2,0,1:T(8,128)}, f32[4,18,8,256]{3,2,0,1:T(8,128)S(1)}, u32[]{:S(2)}) copy-start(f32[4,18,8,256]{3,2,0,1:T(8,128)S(1)} %minimum_add_fusion.27) | copy-start | bytes 1769476
  88.6 4.1 %copy-start.89 = (f32[4,16,8,2]{3,2,0,1:T(8,128)S(1)}, f32[4,16,8,2]{3,2,0,1:T(8,128)}, u32[]{:S(2)}) copy-start(f32[4,16,8,2]{3,2,0,1:T(8,128)} %copy-done.88) | copy-start | bytes 12292
  89.5 3.2 copy-start.87
  119.2 27.8 %collective-permute-start.2 = (f32[4,5,16,2,256]{4,3,0,2,1:T(2,128)}, f32[4,5,16,2,256]{4,3,0,2,1:T(2,128)S(1)}, u32[]{:S(2)}, u32[]{:S(2)}) collective-permute-start(f32[4,5,16,2,256]{4,3,0,2,1:T(2,128)} %get-tuple-element.73), channel_id=1, source_target_pairs={{0,1},{1,2},{2,3},{3,4},{4,5},{5,6},{6,7},{7,0},{8,9},{9,10},{10,1... | collective-permute-start | bytes 1966088 | tf_op jit(solution)/shard_map/ppermute | solution.py:22
  119.5 31.4 %collective-permute-start.3 = (f32[4,5,16,2,256]{4,3,0,2,1:T(2,128)}, f32[4,5,16,2,256]{4,3,0,2,1:T(2,128)}, u32[]{:S(2)}, u32[]{:S(2)}) collective-permute-start(f32[4,5,16,2,256]{4,3,0,2,1:T(2,128)} %get-tuple-element.74), channel_id=1, source_target_pairs={{1,0},{2,1},{3,2},{4,3},{5,4},{6,5},{7,6},{0,7},{9,8},{10,9},{11,1... | collective-permute-start | bytes 1966088 | tf_op jit(solution)/shard_map/ppermute | solution.py:24
  125.7 119.0 %all-to-all-start.1 = ((f32[4,5,16,8,256]{4,3,1,0,2:T(8,128)}), f32[4,5,16,8,256]{4,3,1,0,2:T(8,128)}, u32[]{:S(2)}, u32[]{:S(2)}) async-start(f32[4,5,16,8,256]{4,3,1,0,2:T(8,128)} %copy.120), calls=%async_computation.1 | async-start | bytes 5242880 | tf_op jit(solution)/shard_map/all_to_all | solution.py:170
  153.2 18.8 %copy-start.16 = (f32[4,16,12,256]{3,2,0,1:T(8,128)}, f32[4,16,12,256]{3,2,0,1:T(8,128)S(1)}, u32[]{:S(2)}) copy-start(f32[4,16,12,256]{3,2,0,1:T(8,128)S(1)} %slice_bitcast_fusion.4) | copy-start | bytes 2359300
  153.3 7.6 %copy-start.37 = (f32[4,16,8,256]{3,2,0,1:T(8,128)}, f32[4,16,8,256]{3,2,0,1:T(8,128)S(1)}, u32[]{:S(2)}) copy-start(f32[4,16,8,256]{3,2,0,1:T(8,128)S(1)} %slice.2032) | copy-start | bytes 1572868
  154.2 16.7 %copy-start.12 = (f32[4,16,12,256]{3,2,0,1:T(8,128)}, f32[4,16,12,256]{3,2,0,1:T(8,128)S(1)}, u32[]{:S(2)}) copy-start(f32[4,16,12,256]{3,2,0,1:T(8,128)S(1)} %get-tuple-element.25) | copy-start | bytes 2359300
  154.3 6.6 %copy-start.31 = (f32[4,16,8,256]{3,2,0,1:T(8,128)}, f32[4,16,8,256]{3,2,0,1:T(8,128)S(1)}, u32[]{:S(2)}) copy-start(f32[4,16,8,256]{3,2,0,1:T(8,128)S(1)} %slice.2041) | copy-start | bytes 1572868
  154.4 11.0 %copy-start.2 = (f32[4,16,8,256]{3,2,0,1:T(8,128)}, f32[4,16,8,256]{3,2,0,1:T(8,128)S(1)}, u32[]{:S(2)}) copy-start(f32[4,16,8,256]{3,2,0,1:T(8,128)S(1)} %slice.2054) | copy-start | bytes 1572868
  154.5 6.4 %copy-start.27 = (f32[4,16,8,256]{3,2,0,1:T(8,128)}, f32[4,16,8,256]{3,2,0,1:T(8,128)S(1)}, u32[]{:S(2)}) copy-start(f32[4,16,8,256]{3,2,0,1:T(8,128)S(1)} %slice.2098) | copy-start | bytes 1572868
  154.6 9.2 %copy-start.20 = (f32[4,16,8,256]{3,2,0,1:T(8,128)}, f32[4,16,8,256]{3,2,0,1:T(8,128)S(1)}, u32[]{:S(2)}) copy-start(f32[4,16,8,256]{3,2,0,1:T(8,128)S(1)} %slice.2140) | copy-start | bytes 1572868
  160.3 5.1 %copy-start.6 = (f32[4,18,8,256]{3,2,0,1:T(8,128)}, f32[4,18,8,256]{3,2,0,1:T(8,128)S(1)}, u32[]{:S(2)}) copy-start(f32[4,18,8,256]{3,2,0,1:T(8,128)S(1)} %minimum_add_fusion.22) | copy-start | bytes 1769476
  160.6 3.2 copy-start.35
  170.9 4.1 %copy-start.102 = (f32[4,16,8,1]{3,2,0,1:T(8,128)S(1)}, f32[4,16,8,1]{3,2,0,1:T(8,128)}, u32[]{:S(2)}) copy-start(f32[4,16,8,1]{3,2,0,1:T(8,128)} %get-tuple-element.90) | copy-start | bytes 6148
  176.9 4.5 %copy-start.90 = (f32[4,16,8,2]{3,2,0,1:T(8,128)}, f32[4,16,8,2]{3,2,0,1:T(8,128)S(1)}, u32[]{:S(2)}) copy-start(f32[4,16,8,2]{3,2,0,1:T(8,128)S(1)} %reshape.394) | copy-start | bytes 12292
  186.0 4.5 %copy-start.94 = (f32[4,16,8,2]{3,2,0,1:T(8,128)}, f32[4,16,8,2]{3,2,0,1:T(8,128)S(1)}, u32[]{:S(2)}) copy-start(f32[4,16,8,2]{3,2,0,1:T(8,128)S(1)} %reshape.396) | copy-start | bytes 12292
  212.0 4.1 %copy-start.93 = (f32[4,16,8,2]{3,2,0,1:T(8,128)S(1)}, f32[4,16,8,2]{3,2,0,1:T(8,128)}, u32[]{:S(2)}) copy-start(f32[4,16,8,2]{3,2,0,1:T(8,128)} %copy-done.92) | copy-start | bytes 12292
  233.0 3.3 copy-start.77
  244.7 4.0 %copy-start.103 = (s32[7]{0:T(128)S(1)}, s32[7]{0:T(128)}, u32[]{:S(2)}) copy-start(s32[7]{0:T(128)} %param.3) | copy-start | bytes 88
  244.7 35.2 %all-to-all-start = ((f32[4,5,16,8,256]{4,3,0,1,2:T(8,128)}), f32[4,5,16,8,256]{4,3,0,1,2:T(8,128)S(1)}, u32[]{:S(2)}, u32[]{:S(2)}) async-start(f32[4,5,16,8,256]{4,3,0,1,2:T(8,128)} %copy.116), calls=%async_computation | async-start | bytes 5242880 | tf_op jit(solution)/shard_map/all_to_all | solution.py:171
  289.7 42.1 %collective-permute-start.4 = (f32[8,2,5,4,3,256]{5,0,4,3,2,1:T(8,128)S(1)}, f32[8,2,5,4,3,256]{5,0,4,3,2,1:T(8,128)S(1)}, u32[]{:S(2)}, u32[]{:S(2)}) collective-permute-start(f32[8,2,5,4,3,256]{5,0,4,3,2,1:T(8,128)S(1)} %get-tuple-element.71), channel_id=1, source_target_pairs={{0,1},{1,2},{2,3},{3,4},{4,5},{5,6},{6,7},{7,0},{8,9},{9,10},{10,1... | collective-permute-start | bytes 2949128 | tf_op jit(solution)/shard_map/ppermute | solution.py:22
  289.8 45.5 %collective-permute-start.5 = (f32[8,2,5,4,3,256]{5,0,4,3,2,1:T(8,128)S(1)}, f32[8,2,5,4,3,256]{5,0,4,3,2,1:T(8,128)S(1)}, u32[]{:S(2)}, u32[]{:S(2)}) collective-permute-start(f32[8,2,5,4,3,256]{5,0,4,3,2,1:T(8,128)S(1)} %get-tuple-element.72), channel_id=1, source_target_pairs={{1,0},{2,1},{3,2},{4,3},{5,4},{6,5},{7,6},{0,7},{9,8},{10,9},{11,1... | collective-permute-start | bytes 2949128 | tf_op jit(solution)/shard_map/ppermute | solution.py:24
  (80 other events, 123.8 us)
where the time goes:
time: 400 us; the launch traced here: 394 us
  local copies, waits for them, and re-layouts  113 us (28%)
  waiting for transfers between devices  104 us (26%)
  other arithmetic  104 us (26%)
  blocking collectives  33.8 us (8%)
  starting transfers between devices  24.6 us (6%)
  matrix products  11.2 us (3%)
    ppermute x3, waiting for transfers between devices, extended_2(): lax.ppermute(tail, axis, [(i, (i + 1) % count) for i in range(count)])  78.6 us
    slice x48, local copies, waits for them, and re-layouts, residual(): jnp.pad(component, ((0, 0), (0, 0), (0, 0), (2, 2)), mode='edge')  44.3 us
    sub x20, other arithmetic, divergence(): 0.5 * (left_flux[member] + right_flux[member])  43.9 us
    all_to_all x1, blocking collectives, body(): lax.all_to_all(change_freq, 'inst', split_axis=0, concat_axis=2, tiled=True)  33.8 us
    unnamed x212, local copies, waits for them, and re-layouts  26.6 us
    reshape x20, local copies, waits for them, and re-layouts, residual(): jnp.pad(component, ((0, 0), (0, 0), (0, 0), (2, 2)), mode='edge')  17.8 us
    all_to_all x1, waiting for transfers between devices, body(): lax.all_to_all(second_sweep, 'inst', split_axis=2, concat_axis=0, tiled=T...  16.2 us
    concatenate x10, other arithmetic, residual(): jnp.pad(component, ((0, 0), (0, 0), (0, 0), (2, 2)), mode='edge')  14.2 us
  transfers between devices with their start and end apart: 8, of which 7 were waited for; matrix products, arithmetic and copies ran while one was open for 25% of the time, Pallas kernels for 0%

commit v1 on v0

--- a/solution.py
+++ b/solution.py
@@ -10,6 +10,13 @@
 smooth_weight = 0.5
 base_rate = 0.5
 diagonal_weight = 3.0
+
+
+def trade_parts(block, axis, split, join):
+    devices = lax.axis_size(axis)
+    shards = jnp.stack(jnp.split(block, devices, axis=split), axis=0)
+    shards = lax.all_to_all(shards, axis, split_axis=0, concat_axis=0)
+    return jnp.concatenate(shards, axis=join)
 
 
 def extended_2(cells, sides, width):
@@ -168,7 +175,7 @@
     second_sweep = residual(segmented_ext)
     state_freq, residual_freq = (
         lax.all_to_all(state, "inst", split_axis=2, concat_axis=0, tiled=True),
-        lax.all_to_all(second_sweep, "inst", split_axis=2, concat_axis=0, tiled=True),
+        trade_parts(second_sweep, "inst", 2, 0),
     )
     forward, inverse = transform_tables(NT)
     layout = residual_freq.shape

time: 400 us -> 384 us (0.960)
  other arithmetic: 104 us -> 96 us
  local copies, waits for them, and re-layouts: 113 us -> 106 us
    reshape x20, local copies, waits for them, and re-layouts: 17.8 us -> 10.1 us  [residual(): jnp.pad(component, ((0, 0), (0, 0), (0, 0), (2, 2)), mode='edge')]
    slice x48, local copies, waits for them, and re-layouts: 44.3 us -> 37.7 us  [residual(): jnp.pad(component, ((0, 0), (0, 0), (0, 0), (2, 2)), mode='edge')]
    sub x28, other arithmetic: 10.2 us -> 5.04 us  [divergence(): take_part(component, 1, extent - 1, along)]
    sub x20, other arithmetic: 43.9 us -> 38.9 us  [divergence(): 0.5 * (left_flux[member] + right_flux[member])]
    slice x10, local copies, waits for them, and re-layouts: 0.71 us -> 4.9 us  [residual(): inner = [component[:, :, 2:-2, :] for component in states]]
    unnamed x212 -> x170, local copies, waits for them, and re-layouts: 26.6 us -> 25.5 us
  transfers between devices with their start and end apart: 8 -> 8, of which waited for: 7 -> 7; matrix products, arithmetic and copies ran while one was open for 25% -> 22% of each run, Pallas kernels for 0% -> 0%
where the time goes in v1:
time: 384 us; the launch traced here: 378 us
  local copies, waits for them, and re-layouts  106 us (28%)
  waiting for transfers between devices  104 us (27%)
  other arithmetic  96 us (25%)
  blocking collectives  33.8 us (9%)
  starting transfers between devices  25.1 us (7%)
  matrix products  11 us (3%)
    ppermute x3, waiting for transfers between devices, extended_2(): lax.ppermute(tail, axis, [(i, (i + 1) % count) for i in range(count)])  77.8 us
    sub x20, other arithmetic, divergence(): 0.5 * (left_flux[member] + right_flux[member])  38.9 us
    slice x48, local copies, waits for them, and re-layouts, residual(): jnp.pad(component, ((0, 0), (0, 0), (0, 0), (2, 2)), mode='edge')  37.7 us
    all_to_all x1, blocking collectives, body(): lax.all_to_all(change_freq, 'inst', split_axis=0, concat_axis=2, tiled=True)  33.8 us
    unnamed x170, local copies, waits for them, and re-layouts  25.5 us
    all_to_all x1, waiting for transfers between devices, trade_parts(): shards = lax.all_to_all(shards, axis, split_axis=0, concat_axis=0)  16.3 us
    concatenate x10, other arithmetic, residual(): jnp.pad(component, ((0, 0), (0, 0), (0, 0), (2, 2)), mode='edge')  14.2 us
    add x30, other arithmetic, limited(): jnp.maximum(0.0, jnp.minimum(lower, upper))  13.5 us
  transfers between devices with their start and end apart: 8, of which 7 were waited for; matrix products, arithmetic and copies ran while one was open for 22% of the time, Pallas kernels for 0%

profile of v1, /device:TPU:0, one launch (start us, length us, event | category | flops | bytes accessed | tf_op | source)
XLA Modules:
  0.0 377.7 jit_solution(6455743470994783318)
XLA Ops:
  0.0 3.2 fusion.217
  3.2 3.0 collective-permute-start
  6.2 3.1 collective-permute-start.1
  9.3 24.9 %collective-permute-done = f32[4,5,16,2,256]{4,3,0,2,1:T(2,128)S(1)} collective-permute-done((f32[4,5,16,2,256]{4,3,0,2,1:T(2,128)S(1)}, f32[4,5,16,2,256]{4,3,0,2,1:T(2,128)S(1)}, u32[]{:S(2)}, u32[]{:S(2)}) %collective-permute-start) | collective-permute-done | bytes 655392 | tf_op jit(solution)/shard_map/ppermute | solution.py:29
  34.3 2.2 collective-permute-done.1
  40.4 2.4 multiply_subtract_fusion.26
  93.8 4.1 %multiply_subtract_fusion.16 = (f32[4,16,8,257]{3,2,0,1:T(8,128)S(1)}, f32[4,16,8,257]{3,2,0,1:T(8,128)S(1)}, f32[4,16,8,257]{3,2,0,1:T(8,128)S(1)}, f32[4,16,8,257]{3,2,0,1:T(8,128)S(1)}, f32[4,16,8,257]{3,2,0,1:T(8,128)S(1)}) fusion(f32[4,16,8,258]{3,2,0,1:T(8,128)S(1)} %copy-done.21, f32[4,16,8,256]{3,2,0,1:T(8,128)S(1)} %copy-done.28, ...), kind=kLoop, calls=%fused_computation.255 | loop fusion | flops 8816128 | bytes 10557440 | tf_op jit(solution)/shard_map/sub | solution.py:111
  107.2 3.5 multiply_subtract_fusion.6
  110.8 2.2 multiply_subtract_fusion.7
  120.6 4.4 %collective-permute-start.3 = (f32[4,5,16,2,256]{4,3,0,2,1:T(2,128)}, f32[4,5,16,2,256]{4,3,0,2,1:T(2,128)}, u32[]{:S(2)}, u32[]{:S(2)}) collective-permute-start(f32[4,5,16,2,256]{4,3,0,2,1:T(2,128)} %get-tuple-element.78), channel_id=1, source_target_pairs={{1,0},{2,1},{3,2},{4,3},{5,4},{6,5},{7,6},{0,7},{9,8},{10,9},{11,1... | collective-permute-start | bytes 1966088 | tf_op jit(solution)/shard_map/ppermute | solution.py:31
  126.8 5.3 %all-to-all-start.1 = ((f32[4,5,16,8,256]{4,3,1,0,2:T(8,128)}), f32[4,5,16,8,256]{4,3,1,0,2:T(8,128)}, u32[]{:S(2)}, u32[]{:S(2)}) async-start(f32[4,5,16,8,256]{4,3,1,0,2:T(8,128)} %copy.117), calls=%async_computation.1 | async-start | bytes 5242880 | tf_op jit(solution)/shard_map/all_to_all | solution.py:177
  132.1 16.0 %collective-permute-done.2 = f32[4,5,16,2,256]{4,3,0,2,1:T(2,128)} collective-permute-done((f32[4,5,16,2,256]{4,3,0,2,1:T(2,128)}, f32[4,5,16,2,256]{4,3,0,2,1:T(2,128)}, u32[]{:S(2)}, u32[]{:S(2)}) %collective-permute-start.2) | collective-permute-done | bytes 655392 | tf_op jit(solution)/shard_map/ppermute | solution.py:29
  148.1 3.9 %collective-permute-done.3 = f32[4,5,16,2,256]{4,3,0,2,1:T(2,128)} collective-permute-done((f32[4,5,16,2,256]{4,3,0,2,1:T(2,128)}, f32[4,5,16,2,256]{4,3,0,2,1:T(2,128)}, u32[]{:S(2)}, u32[]{:S(2)}) %collective-permute-start.3) | collective-permute-done | bytes 655392 | tf_op jit(solution)/shard_map/ppermute | solution.py:31
  152.0 2.3 pad_maximum_fusion.1
  199.5 4.1 %multiply_subtract_fusion.11 = (f32[4,16,8,257]{3,2,0,1:T(8,128)S(1)}, f32[4,16,8,257]{3,2,0,1:T(8,128)S(1)}, f32[4,16,8,257]{3,2,0,1:T(8,128)S(1)}, f32[4,16,8,257]{3,2,0,1:T(8,128)S(1)}, f32[4,16,8,257]{3,2,0,1:T(8,128)S(1)}) fusion(f32[4,16,8,258]{3,2,0,1:T(8,128)S(1)} %minimum_add_fusion.11, f32[4,16,8,256]{3,2,0,1:T(8,128)S(1)} %copy-done.26, ...), kind=kLoop, calls=%fused_computation.244 | loop fusion | flops 8816128 | bytes 10557440 | tf_op jit(solution)/shard_map/sub | solution.py:111
  216.7 3.5 multiply_subtract_fusion.1
  220.2 2.4 multiply_subtract_fusion.2
  226.7 3.8 %all-to-all-start = ((f32[4,4,5,4,8,256]{5,4,1,3,2,0:T(8,128)}), f32[4,4,5,4,8,256]{5,4,1,3,2,0:T(8,128)S(1)}, u32[]{:S(2)}, u32[]{:S(2)}) async-start(f32[4,4,5,4,8,256]{5,4,1,3,2,0:T(8,128)} %pad_maximum_fusion.3), calls=%async_computation | async-start | bytes 5242880 | tf_op jit(solution)/shard_map/all_to_all | solution.py:18
  230.7 3.6 copy.147
  234.3 3.0 reshape.404
  237.3 2.5 copy.127
  239.9 3.7 fusion.22
  245.5 16.3 %all-to-all-done = f32[4,4,5,4,8,256]{5,4,1,3,2,0:T(8,128)S(1)} async-done(((f32[4,4,5,4,8,256]{5,4,1,3,2,0:T(8,128)}), f32[4,4,5,4,8,256]{5,4,1,3,2,0:T(8,128)S(1)}, u32[]{:S(2)}, u32[]{:S(2)}) %all-to-all-start) | async-done | bytes 2621472 | tf_op jit(solution)/shard_map/all_to_all | solution.py:18
  267.3 3.7 fusion.21
  271.4 5.1 %collective-permute-start.5 = (f32[8,2,5,4,3,256]{5,0,4,3,2,1:T(8,128)S(1)}, f32[8,2,5,4,3,256]{5,0,4,3,2,1:T(8,128)S(1)}, u32[]{:S(2)}, u32[]{:S(2)}) collective-permute-start(f32[8,2,5,4,3,256]{5,0,4,3,2,1:T(8,128)S(1)} %get-tuple-element.72), channel_id=1, source_target_pairs={{1,0},{2,1},{3,2},{4,3},{5,4},{6,5},{7,6},{0,7},{9,8},{10,9},{11,1... | collective-permute-start | bytes 2949128 | tf_op jit(solution)/shard_map/ppermute | solution.py:31
  276.5 36.9 %collective-permute-done.4 = f32[8,2,5,4,3,256]{5,0,4,3,2,1:T(8,128)S(1)} collective-permute-done((f32[8,2,5,4,3,256]{5,0,4,3,2,1:T(8,128)S(1)}, f32[8,2,5,4,3,256]{5,0,4,3,2,1:T(8,128)S(1)}, u32[]{:S(2)}, u32[]{:S(2)}) %collective-permute-start.4) | collective-permute-done | bytes 983072 | tf_op jit(solution)/shard_map/ppermute | solution.py:29
  313.4 3.5 collective-permute-done.5
  328.7 2.3 copy.120
  331.0 3.2 reshape.405
  334.2 2.5 copy.128
  336.7 3.6 fusion.26
  341.9 33.8 %all_to_all.38 = f32[16,5,4,8,256]{4,3,2,1,0:T(8,128)S(1)} all-to-all(f32[16,5,4,8,256]{4,3,2,1,0:T(8,128)S(1)} %copy.122), channel_id=1, replica_groups=mesh['inst'=4,'blk'=8] {'inst'}, dimensions={0} | all-to-all | bytes 5242880 | tf_op jit(solution)/shard_map/all_to_all | solution.py:202
  (413 shorter events, 157.1 us)
Async XLA Ops:
  0.0 36.5 %copy-start.15 = (f32[4,5,16,8,256]{4,3,2,1,0:T(8,128)S(1)}, f32[4,5,16,8,256]{4,3,2,1,0:T(8,128)}, u32[]{:S(2)}) copy-start(f32[4,5,16,8,256]{4,3,2,1,0:T(8,128)} %param.2) | copy-start | bytes 7864324
  3.2 31.1 %collective-permute-start = (f32[4,5,16,2,256]{4,3,0,2,1:T(2,128)S(1)}, f32[4,5,16,2,256]{4,3,0,2,1:T(2,128)S(1)}, u32[]{:S(2)}, u32[]{:S(2)}) collective-permute-start(f32[4,5,16,2,256]{4,3,0,2,1:T(2,128)S(1)} %get-tuple-element.79), channel_id=1, source_target_pairs={{0,1},{1,2},{2,3},{3,4},{4,5},{5,6},{6,7},{7,0},{8,9},{9,10},{10,1... | collective-permute-start | bytes 1966088 | tf_op jit(solution)/shard_map/ppermute | solution.py:29
  6.2 30.2 %collective-permute-start.1 = (f32[4,5,16,2,256]{4,3,0,2,1:T(2,128)S(1)}, f32[4,5,16,2,256]{4,3,0,2,1:T(2,128)S(1)}, u32[]{:S(2)}, u32[]{:S(2)}) collective-permute-start(f32[4,5,16,2,256]{4,3,0,2,1:T(2,128)S(1)} %get-tuple-element.80), channel_id=1, source_target_pairs={{1,0},{2,1},{3,2},{4,3},{5,4},{6,5},{7,6},{0,7},{9,8},{10,9},{11,1... | collective-permute-start | bytes 1966088 | tf_op jit(solution)/shard_map/ppermute | solution.py:31
  38.5 8.8 %copy-start.7 = (f32[4,16,12,256]{3,2,0,1:T(8,128)}, f32[4,16,12,256]{3,2,0,1:T(8,128)S(1)}, u32[]{:S(2)}) copy-start(f32[4,16,12,256]{3,2,0,1:T(8,128)S(1)} %get-tuple-element.45) | copy-start | bytes 2359300
  38.6 4.3 %copy-start.24 = (f32[4,16,8,256]{3,2,0,1:T(8,128)}, f32[4,16,8,256]{3,2,0,1:T(8,128)S(1)}, u32[]{:S(2)}) copy-start(f32[4,16,8,256]{3,2,0,1:T(8,128)S(1)} %slice.1936) | copy-start | bytes 1572868
  38.7 5.8 %copy-start.17 = (f32[4,16,8,256]{3,2,0,1:T(8,128)}, f32[4,16,8,256]{3,2,0,1:T(8,128)S(1)}, u32[]{:S(2)}) copy-start(f32[4,16,8,256]{3,2,0,1:T(8,128)S(1)} %slice.1978) | copy-start | bytes 1572868
  38.8 5.7 %copy-start.3 = (f32[4,16,8,256]{3,2,0,1:T(8,128)}, f32[4,16,8,256]{3,2,0,1:T(8,128)S(1)}, u32[]{:S(2)}) copy-start(f32[4,16,8,256]{3,2,0,1:T(8,128)S(1)} %slice.1892) | copy-start | bytes 1572868
  39.0 9.5 %copy-start.13 = (f32[4,16,12,256]{3,2,0,1:T(8,128)}, f32[4,16,12,256]{3,2,0,1:T(8,128)S(1)}, u32[]{:S(2)}) copy-start(f32[4,16,12,256]{3,2,0,1:T(8,128)S(1)} %slice_bitcast_fusion.9) | copy-start | bytes 2359300
  39.4 5.1 %copy-start.5 = (f32[4,18,8,256]{3,2,0,1:T(8,128)}, f32[4,18,8,256]{3,2,0,1:T(8,128)S(1)}, u32[]{:S(2)}) copy-start(f32[4,18,8,256]{3,2,0,1:T(8,128)S(1)} %minimum_add_fusion.27) | copy-start | bytes 1769476
  54.0 2.9 copy-start.36
  88.1 4.1 %copy-start.61 = (f32[4,16,8,2]{3,2,0,1:T(8,128)S(1)}, f32[4,16,8,2]{3,2,0,1:T(8,128)}, u32[]{:S(2)}) copy-start(f32[4,16,8,2]{3,2,0,1:T(8,128)} %copy-done.60) | copy-start | bytes 12292
  89.0 3.2 copy-start.59
  90.0 2.2 copy-start.33
  90.0 2.2 copy-start.48
  90.0 2.2 copy-start.55
  91.6 2.2 copy-start.37
  120.3 27.8 %collective-permute-start.2 = (f32[4,5,16,2,256]{4,3,0,2,1:T(2,128)}, f32[4,5,16,2,256]{4,3,0,2,1:T(2,128)}, u32[]{:S(2)}, u32[]{:S(2)}) collective-permute-start(f32[4,5,16,2,256]{4,3,0,2,1:T(2,128)} %get-tuple-element.77), channel_id=1, source_target_pairs={{0,1},{1,2},{2,3},{3,4},{4,5},{5,6},{6,7},{7,0},{8,9},{9,10},{10,1... | collective-permute-start | bytes 1966088 | tf_op jit(solution)/shard_map/ppermute | solution.py:29
  120.6 31.4 %collective-permute-start.3 = (f32[4,5,16,2,256]{4,3,0,2,1:T(2,128)}, f32[4,5,16,2,256]{4,3,0,2,1:T(2,128)}, u32[]{:S(2)}, u32[]{:S(2)}) collective-permute-start(f32[4,5,16,2,256]{4,3,0,2,1:T(2,128)} %get-tuple-element.78), channel_id=1, source_target_pairs={{1,0},{2,1},{3,2},{4,3},{5,4},{6,5},{7,6},{0,7},{9,8},{10,9},{11,1... | collective-permute-start | bytes 1966088 | tf_op jit(solution)/shard_map/ppermute | solution.py:31
  126.8 25.2 %copy-start.30 = (f32[4,5,16,8,256]{4,3,0,2,1:T(8,128)S(1)}, f32[4,5,16,8,256]{4,3,0,2,1:T(8,128)}, u32[]{:S(2)}) copy-start(f32[4,5,16,8,256]{4,3,0,2,1:T(8,128)} %copy-done.29) | copy-start | bytes 7864324
  126.8 99.9 %all-to-all-start.1 = ((f32[4,5,16,8,256]{4,3,1,0,2:T(8,128)}), f32[4,5,16,8,256]{4,3,1,0,2:T(8,128)}, u32[]{:S(2)}, u32[]{:S(2)}) async-start(f32[4,5,16,8,256]{4,3,1,0,2:T(8,128)} %copy.117), calls=%async_computation.1 | async-start | bytes 5242880 | tf_op jit(solution)/shard_map/all_to_all | solution.py:177
  154.4 8.2 %copy-start.11 = (f32[4,16,12,256]{3,2,0,1:T(8,128)}, f32[4,16,12,256]{3,2,0,1:T(8,128)S(1)}, u32[]{:S(2)}) copy-start(f32[4,16,12,256]{3,2,0,1:T(8,128)S(1)} %slice_bitcast_fusion.4) | copy-start | bytes 2359300
  157.0 8.2 %copy-start.9 = (f32[4,16,12,256]{3,2,0,1:T(8,128)}, f32[4,16,12,256]{3,2,0,1:T(8,128)S(1)}, u32[]{:S(2)}) copy-start(f32[4,16,12,256]{3,2,0,1:T(8,128)S(1)} %get-tuple-element.25) | copy-start | bytes 2359300
  182.9 3.0 copy-start.34
  195.4 2.5 copy-start.69
  195.5 2.4 copy-start.67
  195.7 2.2 copy-start.46
  195.7 2.2 copy-start.47
  195.7 2.2 copy-start.65
  226.7 3.8 %copy-start.82 = (s32[7]{0:T(128)S(1)}, s32[7]{0:T(128)}, u32[]{:S(2)}) copy-start(s32[7]{0:T(128)} %param.3) | copy-start | bytes 88
  226.7 35.0 %all-to-all-start = ((f32[4,4,5,4,8,256]{5,4,1,3,2,0:T(8,128)}), f32[4,4,5,4,8,256]{5,4,1,3,2,0:T(8,128)S(1)}, u32[]{:S(2)}, u32[]{:S(2)}) async-start(f32[4,4,5,4,8,256]{5,4,1,3,2,0:T(8,128)} %pad_maximum_fusion.3), calls=%async_computation | async-start | bytes 5242880 | tf_op jit(solution)/shard_map/all_to_all | solution.py:18
  271.3 42.1 %collective-permute-start.4 = (f32[8,2,5,4,3,256]{5,0,4,3,2,1:T(8,128)S(1)}, f32[8,2,5,4,3,256]{5,0,4,3,2,1:T(8,128)S(1)}, u32[]{:S(2)}, u32[]{:S(2)}) collective-permute-start(f32[8,2,5,4,3,256]{5,0,4,3,2,1:T(8,128)S(1)} %get-tuple-element.71), channel_id=1, source_target_pairs={{0,1},{1,2},{2,3},{3,4},{4,5},{5,6},{6,7},{7,0},{8,9},{9,10},{10,1... | collective-permute-start | bytes 2949128 | tf_op jit(solution)/shard_map/ppermute | solution.py:29
  271.4 45.5 %collective-permute-start.5 = (f32[8,2,5,4,3,256]{5,0,4,3,2,1:T(8,128)S(1)}, f32[8,2,5,4,3,256]{5,0,4,3,2,1:T(8,128)S(1)}, u32[]{:S(2)}, u32[]{:S(2)}) collective-permute-start(f32[8,2,5,4,3,256]{5,0,4,3,2,1:T(8,128)S(1)} %get-tuple-element.72), channel_id=1, source_target_pairs={{1,0},{2,1},{3,2},{4,3},{5,4},{6,5},{7,6},{0,7},{9,8},{10,9},{11,1... | collective-permute-start | bytes 2949128 | tf_op jit(solution)/shard_map/ppermute | solution.py:31
  (59 other events, 78.0 us)
